TPU v7x, 32 devices: a whole 2x2x4 slice. The times are simulated.
32 devices in a mesh: dp: 2 (over x), expert: 16 (over z, y, core).
Axes of the slice: x: 2, y: 2, z: 4, core: 2. Of those that a mesh axis runs over, the one named last changes fastest.
Arguments:
- gradients: bfloat16 [16, 1024, 5888], P(None, ('dp', 'expert')), may hold values from -6 to 6
- momentum: bfloat16 [16, 1024, 5888], P('expert', 'dp'), may hold values from -6 to 6
- right_factor: bfloat16 [16, 5888, 256], P('expert', 'dp'), may hold values from -6 to 6
Outputs:
- new_momentum: bfloat16 [16, 1024, 5888], P('expert', 'dp')
- new_factor: bfloat16 [16, 5888, 256], P('expert', 'dp')
- update_rows: bfloat16 [16, 1024, 5888], P(None, ('dp', 'expert'))
All inputs are finite; a program needn't handle non-finite values.
Results may differ from a plain program's by a relative error of at most 0.009.
Values may be sent and summed in bfloat16 or wider, within the bound.
A program may use at most 128 MiB of HBM per device.

v0:
```python
import math
import jax
import jax.numpy as jnp
from jax import lax
from jax.sharding import PartitionSpec as P

D = 5888
FFW = 1024
RANK = 256
decay_rate = 0.95
epsilon = 1e-06


def body(gradients, momentum, right_factor):
    arrived = lax.all_to_all(gradients, "expert", split_axis=0, concat_axis=1, tiled=True)
    rank_cols = right_factor.shape[2]
    blended = (
        decay_rate * momentum[0].astype(jnp.float32) + arrived[0].astype(jnp.float32)
    ).astype(jnp.bfloat16)
    columns = blended
    left = jnp.dot(
        columns,
        lax.all_gather(right_factor[0], "dp", axis=0, tiled=True),
        preferred_element_type=jnp.float32,
    )
    gram_matrix = lax.psum(jnp.dot(left.T, left, precision=lax.Precision.HIGHEST), "dp")
    lower = jnp.linalg.cholesky(gram_matrix)
    inverse = jax.scipy.linalg.solve_triangular(
        lower, jnp.eye(rank_cols, dtype=jnp.float32), lower=True
    )
    ortho = jnp.dot(left, inverse.T, precision=lax.Precision.HIGHEST).astype(jnp.bfloat16)
    columns = blended
    right_half = lax.psum_scatter(
        lax.dot_general(
            columns, ortho, (((0,), (0,)), ((), ())), preferred_element_type=jnp.float32
        ),
        "dp",
        scatter_dimension=0,
        tiled=True,
    )
    column = lax.psum(jnp.sum(right_half * right_half, axis=0), "dp")
    own_factor = (right_half * lax.rsqrt(column / D + epsilon)).astype(jnp.bfloat16)
    right_rounded = lax.all_gather(right_half.astype(jnp.bfloat16), "dp", axis=0, tiled=True)
    full_factor = lax.all_gather(own_factor, "dp", axis=0, tiled=True)
    kept = (
        blended.astype(jnp.float32)
        - (1.0 - decay_rate)
        * lax.dot_general(
            ortho, right_rounded, (((1,), (1,)), ((), ())), preferred_element_type=jnp.float32
        )
    ).astype(jnp.bfloat16)
    update = (
        math.sqrt(FFW / RANK)
        * lax.dot_general(
            ortho, full_factor, (((1,), (1,)), ((), ())), preferred_element_type=jnp.float32
        )
    ).astype(jnp.bfloat16)
    moments = [kept]
    factors = [own_factor]
    updates = [update]
    returned = lax.all_to_all(jnp.stack(updates), "expert", split_axis=1, concat_axis=0, tiled=True)
    return (jnp.stack(moments), jnp.stack(factors), returned)


def solution(mesh):
    in_specs = (P(None, ("dp", "expert"), None), P("expert", "dp", None), P("expert", "dp", None))
    out_specs = (P("expert", "dp", None), P("expert", "dp", None), P(None, ("dp", "expert"), None))
    return jax.shard_map(body, mesh=mesh, in_specs=in_specs, out_specs=out_specs, check_vma=False)
```

profile of v0, /device:TPU:13, one launch (start us, length us, event | category | flops | bytes accessed | tf_op | source)
XLA Modules:
  0.0 616.2 jit_solution(494227464245584876)
XLA Ops:
  7.2 6.5 %all-to-all-start = ((bf16[16,32,5888]{2,1,0:T(8,128)(2,1)}), bf16[16,32,5888]{2,1,0:T(8,128)(2,1)}, u32[]{:S(2)}, u32[]{:S(2)}) async-start(bf16[16,32,5888]{2,1,0:T(8,128)(2,1)} %param.3), calls=%async_computation | async-start | bytes 12058624 | tf_op jit(solution)/shard_map/all_to_all | solution.py:15
  14.5 131.0 %all-to-all-done = bf16[16,32,5888]{2,1,0:T(8,128)(2,1)} async-done(((bf16[16,32,5888]{2,1,0:T(8,128)(2,1)}), bf16[16,32,5888]{2,1,0:T(8,128)(2,1)}, u32[]{:S(2)}, u32[]{:S(2)}) %all-to-all-start) | async-done | bytes 6029344 | tf_op jit(solution)/shard_map/all_to_all | solution.py:15
  145.5 8.9 %fusion = bf16[512,5888]{1,0:T(8,128)(2,1)} fusion(bf16[1,512,5888]{2,1,0:T(8,128)(2,1)} %param.4, bf16[16,32,5888]{2,1,0:T(8,128)(2,1)} %all-to-all-done), kind=kLoop, calls=%fused_computation.3 | loop fusion | flops 15073280 | bytes 18087936 | tf_op jit(solution)/shard_map/convert_element_type | solution.py:19
  154.3 5.3 fusion.3
  159.7 1.7 fusion.18
  161.7 22.1 %all-reduce.3.cloned.1.call-done = f32[256,256]{0,1:T(8,128)} async-done(((f32[256,256]{0,1:T(8,128)}), f32[256,256]{0,1:T(8,128)}) %all-reduce.3.cloned.1.call-update) | async-done | bytes 262160 | tf_op jit(solution)/shard_map/psum | solution.py:26
  183.8 1.1 copy.12
  184.8 1.0 fusion.8
  185.8 11.7 %cholesky.50 = f32[128,128]{1,0:T(8,128)S(1)} custom-call(f32[128,128]{1,0:T(8,128)S(1)} %cholesky.118), custom_call_target="Cholesky" | custom-call | tf_op jit(solution)/shard_map/jit(cholesky)/cholesky | solution.py:27
  197.6 9.8 %custom-call.15 = f32[1,128,128]{1,2,0:T(8,128)S(1)} custom-call(f32[1,128,128]{2,1,0:T(8,128)S(1)} %get-tuple-element.26), custom_call_target="InvertDiagBlocksLowerTriangular" | custom-call | tf_op jit(solution)/shard_map/jit(cholesky)/cholesky | solution.py:27
  207.9 11.7 %cholesky.105 = f32[128,128]{1,0:T(8,128)S(1)} custom-call(f32[128,128]{1,0:T(8,128)S(1)} %convolution_subtract_fusion.1), custom_call_target="Cholesky" | custom-call | tf_op jit(solution)/shard_map/jit(cholesky)/cholesky | solution.py:27
  219.7 0.7 compare_reduce_fusion
  221.8 4.3 while.1
  222.6 1.4 bitcast_dynamic-update-slice_fusion.2
  224.7 1.4 bitcast_dynamic-update-slice_fusion.2
  226.1 19.7 %custom-call.16 = f32[2,128,128]{1,2,0:T(8,128)S(1)} custom-call(f32[2,128,128]{2,1,0:T(8,128)S(1)} %get-tuple-element.10), custom_call_target="InvertDiagBlocksLowerTriangular" | custom-call | tf_op jit(solution)/shard_map/jit(_solve_triangular)/triangular_solve | solution.py:28
  247.3 7.1 %fusion.19 = f32[5888,256]{1,0:T(8,128)} fusion(bf16[512,5888]{1,0:T(8,128)(2,1)} %fusion, bf16[512,256]{1,0:T(8,128)(2,1)S(1)} %convolution_convert_fusion), kind=kOutput, calls=%fused_computation.47 | convolution fusion | flops 1543503872 | bytes 12320768 | tf_op jit(solution)/shard_map/dot_general | solution.py:34
  254.5 74.7 %reduce-scatter.2.cloned.1.call-done = f32[2944,256]{1,0:T(8,128)} async-done(((f32[5888,256]{1,0:T(8,128)}), f32[2944,256]{1,0:T(8,128)}) %reduce-scatter.2.cloned.1.call-update) | async-done | bytes 3014672 | tf_op jit(solution)/shard_map/reduce_scatter | solution.py:33
  329.2 2.3 multiply_reduce_fusion
  331.5 3.8 psum.15
  335.2 4.8 multiply_convert_fusion.1
  340.0 44.8 %all-gather.7.cloned.1.call-done = bf16[5888,256]{1,0:T(8,128)(2,1)} async-done(((bf16[2944,256]{1,0:T(8,128)(2,1)}), bf16[5888,256]{1,0:T(8,128)(2,1)}) %all-gather.7.cloned.1.call-update) | async-done | bytes 3014672 | tf_op jit(solution)/shard_map/all_gather | solution.py:44
  384.8 3.6 fusion.2
  388.4 10.8 %copy.17 = bf16[1,512,5888]{2,0,1:T(2,128)(2,1)} copy(bf16[1,512,5888]{2,1,0:T(8,128)(2,1)S(1)} %fusion.2) | data formatting | bytes 12058624 | tf_op jit(solution)/shard_map/stack | solution.py:61
  399.8 38.3 %reduce.12 = bf16[512,5888]{1,0:T(8,128)(2,1)} reduce(bf16[512,1,5888]{2,1,0:T(2,128)(2,1)} %bitcast.60, bf16[]{:T(256)} %broadcast.118), dimensions={1}, to_apply=%bitcast.52.reduce_sub_computation | reduce | bytes 12058626
  438.1 11.3 %reshape.59 = bf16[16,2,94208]{2,1,0:T(2,128)(2,1)} reshape(bf16[512,5888]{1,0:T(8,128)(2,1)} %reduce.12) | data formatting | bytes 12058624
  449.5 6.5 %all-to-all-start.1 = ((bf16[16,2,94208]{2,1,0:T(2,128)(2,1)}), bf16[16,2,94208]{2,1,0:T(2,128)(2,1)}, u32[]{:S(2)}, u32[]{:S(2)}) async-start(bf16[16,2,94208]{2,1,0:T(2,128)(2,1)} %reshape.59), calls=%async_computation.2 | async-start | bytes 12058624 | tf_op jit(solution)/shard_map/all_to_all | solution.py:61
  456.6 44.4 %all-gather.5.cloned.1.call-done = bf16[5888,256]{1,0:T(8,128)(2,1)} async-done(((bf16[2944,256]{1,0:T(8,128)(2,1)}), bf16[5888,256]{1,0:T(8,128)(2,1)}) %all-gather.5.cloned.1.call-update) | async-done | bytes 3014672 | tf_op jit(solution)/shard_map/all_gather | solution.py:43
  501.0 8.0 %fusion.1 = bf16[1,512,5888]{2,1,0:T(8,128)(2,1)} fusion(bf16[512,256]{1,0:T(8,128)(2,1)S(1)} %convolution_convert_fusion, bf16[5888,256]{1,0:T(8,128)(2,1)} %all-gather.5.cloned.1.call-done, bf16[512,5888]{1,0:T(8,128)(2,1)} %fusion), kind=kOutput, calls=%fused_computation.6 | convolution fusion | flops 1555562496 | bytes 15335424 | tf_op jit(solution)/shard_map/dot_general | solution.py:48
  509.0 78.8 %all-to-all-done.1 = bf16[16,2,94208]{2,1,0:T(2,128)(2,1)} async-done(((bf16[16,2,94208]{2,1,0:T(2,128)(2,1)}), bf16[16,2,94208]{2,1,0:T(2,128)(2,1)}, u32[]{:S(2)}, u32[]{:S(2)}) %all-to-all-start.1) | async-done | bytes 6029344 | tf_op jit(solution)/shard_map/all_to_all | solution.py:61
  587.8 14.0 %reshape.60 = bf16[512,1,5888]{2,1,0:T(2,128)(2,1)} reshape(bf16[16,2,94208]{2,1,0:T(2,128)(2,1)} %all-to-all-done.1) | data formatting | bytes 12058624
  601.8 7.9 %copy.15 = bf16[1,512,5888]{2,1,0:T(8,128)(2,1)} copy(bf16[1,512,5888]{2,0,1:T(2,128)(2,1)} %bitcast.59) | data formatting | bytes 12058624
  (32 shorter events, 5.6 us)
Async XLA Ops:
  7.2 138.3 %all-to-all-start = ((bf16[16,32,5888]{2,1,0:T(8,128)(2,1)}), bf16[16,32,5888]{2,1,0:T(8,128)(2,1)}, u32[]{:S(2)}, u32[]{:S(2)}) async-start(bf16[16,32,5888]{2,1,0:T(8,128)(2,1)} %param.3), calls=%async_computation | async-start | bytes 12058624 | tf_op jit(solution)/shard_map/all_to_all | solution.py:15
  13.7 140.6 %all-gather.9.cloned.1.call-start = ((), (), s32[]{:S(2)}) async-start(), calls=%async_computation.7 | async-start | bytes 4521984 | tf_op jit(solution)/shard_map/all_gather | solution.py:23
  14.4 169.3 %all-reduce.3.cloned.1.call-start = ((), (), s32[]{:S(2)}) async-start(), calls=%async_computation.3 | async-start | bytes 524288 | tf_op jit(solution)/shard_map/psum | solution.py:26
  161.4 167.8 %reduce-scatter.2.cloned.1.call-start = ((), (), s32[]{:S(2)}) async-start(), calls=%async_computation.4 | async-start | bytes 9043968 | tf_op jit(solution)/shard_map/reduce_scatter | solution.py:33
  254.4 130.4 %all-gather.7.cloned.1.call-start = ((), (), s32[]{:S(2)}) async-start(), calls=%async_computation.6 | async-start | bytes 4521984 | tf_op jit(solution)/shard_map/all_gather | solution.py:44
  449.5 138.3 %all-to-all-start.1 = ((bf16[16,2,94208]{2,1,0:T(2,128)(2,1)}), bf16[16,2,94208]{2,1,0:T(2,128)(2,1)}, u32[]{:S(2)}, u32[]{:S(2)}) async-start(bf16[16,2,94208]{2,1,0:T(2,128)(2,1)} %reshape.59), calls=%async_computation.2 | async-start | bytes 12058624 | tf_op jit(solution)/shard_map/all_to_all | solution.py:61
  456.0 45.0 %all-gather.5.cloned.1.call-start = ((), (), s32[]{:S(2)}) async-start(), calls=%async_computation.5 | async-start | bytes 4521984 | tf_op jit(solution)/shard_map/all_gather | solution.py:43
Sparse Core Ops, SparseCore 0:
  16.0 43.8 all-gather.8
  161.5 22.1 all-reduce.2
  254.5 74.6 reduce-scatter.1
  340.2 44.5 all-gather.6
  458.0 42.9 all-gather.4
where the time goes:
time: 617 us; the launch traced here: 616 us
  waiting for transfers between devices  397 us (64%)
  other arithmetic  109 us (18%)
  local copies, waits for them, and re-layouts  49.9 us (8%)
  matrix products  27.7 us (4%)
  between operations  15.3 us (2%)
  starting transfers between devices  13.7 us (2%)
    all_to_all x1, waiting for transfers between devices, body(): lax.all_to_all(gradients, 'expert', split_axis=0, concat_axis=1, tiled=True)  131 us
    all_to_all x1, waiting for transfers between devices, body(): lax.all_to_all(jnp.stack(updates), 'expert', split_axis=1, concat_axis=0,...  78.8 us
    reduce_scatter x1, waiting for transfers between devices, body(): lax.psum_scatter(lax.dot_general(columns, ortho, (((0,), (0,)), ((), ()))...  74.7 us
    all_gather x1, waiting for transfers between devices, body(): full_factor = lax.all_gather(own_factor, 'dp', axis=0, tiled=True)  44.8 us
    all_gather x1, waiting for transfers between devices, body(): lax.all_gather(right_half.astype(jnp.bfloat16), 'dp', axis=0, tiled=True)  44.4 us
    unnamed x2, other arithmetic  38.3 us
    another operation x6, other arithmetic, body(): lower = jnp.linalg.cholesky(gram_matrix)  34 us
    unnamed x4, local copies, waits for them, and re-layouts  33.8 us
  transfers between devices with their start and end apart: 7, of which 6 were waited for; matrix products, arithmetic and copies ran while one was open for 3% of the time, Pallas kernels for 0%

commit v1 on v0

--- a/solution.py
+++ b/solution.py
@@ -41,7 +41,9 @@
     column = lax.psum(jnp.sum(right_half * right_half, axis=0), "dp")
     own_factor = (right_half * lax.rsqrt(column / D + epsilon)).astype(jnp.bfloat16)
     right_rounded = lax.all_gather(right_half.astype(jnp.bfloat16), "dp", axis=0, tiled=True)
-    full_factor = lax.all_gather(own_factor, "dp", axis=0, tiled=True)
+    full_factor = jnp.concatenate(
+        lax.all_to_all(jnp.stack([own_factor] * lax.axis_size("dp")), "dp", 0, 0), axis=0
+    )
     kept = (
         blended.astype(jnp.float32)
         - (1.0 - decay_rate)

time: 617 us -> 608 us (0.985)
  waiting for transfers between devices: 397 us -> 352 us
  blocking collectives: 3.77 us -> 39.2 us
    all_gather x1 -> x0, waiting for transfers between devices: 44.8 us -> none  [body(): full_factor = lax.all_gather(own_factor, 'dp', axis=0, tiled=True)]
    all_to_all x0 -> x1, blocking collectives: none -> 35.4 us  [body(): lax.all_to_all(jnp.stack([own_factor] * lax.axis_size('dp')), 'dp', 0, 0)]
    unnamed x4 -> x6, local copies, waits for them, and re-layouts: 33.8 us -> 33.8 us
  transfers between devices with their start and end apart: 7 -> 6, of which waited for: 6 -> 5; matrix products, arithmetic and copies ran while one was open for 3% -> 3% of each run, Pallas kernels for 0% -> 0%
where the time goes in v1:
time: 608 us; the launch traced here: 607 us
  waiting for transfers between devices  352 us (58%)
  other arithmetic  109 us (18%)
  local copies, waits for them, and re-layouts  49.9 us (8%)
  blocking collectives  39.2 us (6%)
  matrix products  25.8 us (4%)
  starting transfers between devices  15.4 us (3%)
  between operations  15.3 us (3%)
    all_to_all x1, waiting for transfers between devices, body(): lax.all_to_all(gradients, 'expert', split_axis=0, concat_axis=1, tiled=True)  131 us
    all_to_all x1, waiting for transfers between devices, body(): lax.all_to_all(jnp.stack(updates), 'expert', split_axis=1, concat_axis=0,...  78.8 us
    reduce_scatter x1, waiting for transfers between devices, body(): lax.psum_scatter(lax.dot_general(columns, ortho, (((0,), (0,)), ((), ()))...  74.8 us
    all_gather x1, waiting for transfers between devices, body(): lax.all_gather(right_half.astype(jnp.bfloat16), 'dp', axis=0, tiled=True)  44.4 us
    unnamed x2, other arithmetic  38.3 us
    all_to_all x1, blocking collectives, body(): lax.all_to_all(jnp.stack([own_factor] * lax.axis_size('dp')), 'dp', 0, 0)  35.4 us
    another operation x6, other arithmetic, body(): lower = jnp.linalg.cholesky(gram_matrix)  34 us
    unnamed x6, local copies, waits for them, and re-layouts  33.8 us
  transfers between devices with their start and end apart: 6, of which 5 were waited for; matrix products, arithmetic and copies ran while one was open for 3% of the time, Pallas kernels for 0%

profile of v1, /device:TPU:13, one launch (start us, length us, event | category | flops | bytes accessed | tf_op | source)
XLA Modules:
  0.0 606.8 jit_solution(17346674337146529898)
XLA Ops:
  7.2 6.5 %all-to-all-start = ((bf16[16,32,5888]{2,1,0:T(8,128)(2,1)}), bf16[16,32,5888]{2,1,0:T(8,128)(2,1)}, u32[]{:S(2)}, u32[]{:S(2)}) async-start(bf16[16,32,5888]{2,1,0:T(8,128)(2,1)} %param.3), calls=%async_computation | async-start | bytes 12058624 | tf_op jit(solution)/shard_map/all_to_all | solution.py:15
  14.5 131.0 %all-to-all-done = bf16[16,32,5888]{2,1,0:T(8,128)(2,1)} async-done(((bf16[16,32,5888]{2,1,0:T(8,128)(2,1)}), bf16[16,32,5888]{2,1,0:T(8,128)(2,1)}, u32[]{:S(2)}, u32[]{:S(2)}) %all-to-all-start) | async-done | bytes 6029344 | tf_op jit(solution)/shard_map/all_to_all | solution.py:15
  145.5 8.9 %fusion = bf16[512,5888]{1,0:T(8,128)(2,1)} fusion(bf16[1,512,5888]{2,1,0:T(8,128)(2,1)} %param.4, bf16[16,32,5888]{2,1,0:T(8,128)(2,1)} %all-to-all-done), kind=kLoop, calls=%fused_computation.3 | loop fusion | flops 15073280 | bytes 18087936 | tf_op jit(solution)/shard_map/convert_element_type | solution.py:19
  154.3 5.3 fusion.3
  159.7 1.7 fusion.19
  161.7 22.1 %all-reduce.3.cloned.1.call-done = f32[256,256]{0,1:T(8,128)} async-done(((f32[256,256]{0,1:T(8,128)}), f32[256,256]{0,1:T(8,128)}) %all-reduce.3.cloned.1.call-update) | async-done | bytes 262160 | tf_op jit(solution)/shard_map/psum | solution.py:26
  183.8 1.1 copy.12
  184.8 1.0 fusion.9
  185.8 11.7 %cholesky.50 = f32[128,128]{1,0:T(8,128)S(1)} custom-call(f32[128,128]{1,0:T(8,128)S(1)} %cholesky.118), custom_call_target="Cholesky" | custom-call | tf_op jit(solution)/shard_map/jit(cholesky)/cholesky | solution.py:27
  197.6 9.8 %custom-call.15 = f32[1,128,128]{1,2,0:T(8,128)S(1)} custom-call(f32[1,128,128]{2,1,0:T(8,128)S(1)} %get-tuple-element.26), custom_call_target="InvertDiagBlocksLowerTriangular" | custom-call | tf_op jit(solution)/shard_map/jit(cholesky)/cholesky | solution.py:27
  207.9 11.7 %cholesky.105 = f32[128,128]{1,0:T(8,128)S(1)} custom-call(f32[128,128]{1,0:T(8,128)S(1)} %convolution_subtract_fusion.1), custom_call_target="Cholesky" | custom-call | tf_op jit(solution)/shard_map/jit(cholesky)/cholesky | solution.py:27
  219.7 0.7 compare_reduce_fusion
  221.8 4.3 while.1
  222.6 1.4 bitcast_dynamic-update-slice_fusion.2
  224.7 1.4 bitcast_dynamic-update-slice_fusion.2
  226.1 19.7 %custom-call.16 = f32[2,128,128]{1,2,0:T(8,128)S(1)} custom-call(f32[2,128,128]{2,1,0:T(8,128)S(1)} %get-tuple-element.10), custom_call_target="InvertDiagBlocksLowerTriangular" | custom-call | tf_op jit(solution)/shard_map/jit(_solve_triangular)/triangular_solve | solution.py:28
  247.3 7.1 %fusion.20 = f32[5888,256]{1,0:T(8,128)} fusion(bf16[512,5888]{1,0:T(8,128)(2,1)} %fusion, bf16[512,256]{1,0:T(8,128)(2,1)S(1)} %convolution_convert_fusion), kind=kOutput, calls=%fused_computation.49 | convolution fusion | flops 1543503872 | bytes 12320768 | tf_op jit(solution)/shard_map/dot_general | solution.py:34
  254.4 74.8 %reduce-scatter.2.cloned.1.call-done = f32[2944,256]{1,0:T(8,128)} async-done(((f32[5888,256]{1,0:T(8,128)}), f32[2944,256]{1,0:T(8,128)}) %reduce-scatter.2.cloned.1.call-update) | async-done | bytes 3014672 | tf_op jit(solution)/shard_map/reduce_scatter | solution.py:33
  329.2 2.3 multiply_reduce_fusion
  331.5 3.8 psum.15
  335.2 4.3 fusion.5
  339.8 35.4 %all_to_all.26 = bf16[2,2944,256]{2,1,0:T(8,128)(2,1)S(1)} all-to-all(bf16[2,2944,256]{2,1,0:T(8,128)(2,1)S(1)} %pad_maximum_fusion), channel_id=1, replica_groups=mesh['dp'=2,'expert'=16] {'dp'}, dimensions={0} | all-to-all | bytes 6029312 | tf_op jit(solution)/shard_map/all_to_all | solution.py:45
  375.2 1.8 fusion.2
  377.0 10.8 %copy.17 = bf16[1,512,5888]{2,0,1:T(2,128)(2,1)} copy(bf16[1,512,5888]{2,1,0:T(8,128)(2,1)S(1)} %fusion.2) | data formatting | bytes 12058624 | tf_op jit(solution)/shard_map/stack | solution.py:63
  388.4 38.3 %reduce.12 = bf16[512,5888]{1,0:T(8,128)(2,1)} reduce(bf16[512,1,5888]{2,1,0:T(2,128)(2,1)} %bitcast.62, bf16[]{:T(256)} %broadcast.118), dimensions={1}, to_apply=%bitcast.54.reduce_sub_computation | reduce | bytes 12058626
  426.7 11.3 %reshape.63 = bf16[16,2,94208]{2,1,0:T(2,128)(2,1)} reshape(bf16[512,5888]{1,0:T(8,128)(2,1)} %reduce.12) | data formatting | bytes 12058624
  438.1 8.5 %all-to-all-start.2 = ((bf16[16,2,94208]{2,1,0:T(2,128)(2,1)}), bf16[16,2,94208]{2,1,0:T(2,128)(2,1)}, u32[]{:S(2)}, u32[]{:S(2)}) async-start(bf16[16,2,94208]{2,1,0:T(2,128)(2,1)} %reshape.63), calls=%async_computation.3 | async-start | bytes 12058624 | tf_op jit(solution)/shard_map/all_to_all | solution.py:63
  447.2 44.4 %all-gather.4.cloned.1.call-done = bf16[5888,256]{1,0:T(8,128)(2,1)} async-done(((bf16[2944,256]{1,0:T(8,128)(2,1)}), bf16[5888,256]{1,0:T(8,128)(2,1)}) %all-gather.4.cloned.1.call-update) | async-done | bytes 3014672 | tf_op jit(solution)/shard_map/all_gather | solution.py:43
  491.6 8.0 %fusion.1 = bf16[1,512,5888]{2,1,0:T(8,128)(2,1)} fusion(bf16[512,256]{1,0:T(8,128)(2,1)S(1)} %convolution_convert_fusion, bf16[5888,256]{1,0:T(8,128)(2,1)} %all-gather.4.cloned.1.call-done, bf16[512,5888]{1,0:T(8,128)(2,1)} %fusion), kind=kOutput, calls=%fused_computation.6 | convolution fusion | flops 1555562496 | bytes 15335424 | tf_op jit(solution)/shard_map/dot_general | solution.py:50
  499.6 78.8 %all-to-all-done.2 = bf16[16,2,94208]{2,1,0:T(2,128)(2,1)} async-done(((bf16[16,2,94208]{2,1,0:T(2,128)(2,1)}), bf16[16,2,94208]{2,1,0:T(2,128)(2,1)}, u32[]{:S(2)}, u32[]{:S(2)}) %all-to-all-start.2) | async-done | bytes 6029344 | tf_op jit(solution)/shard_map/all_to_all | solution.py:63
  578.4 14.0 %reshape.64 = bf16[512,1,5888]{2,1,0:T(2,128)(2,1)} reshape(bf16[16,2,94208]{2,1,0:T(2,128)(2,1)} %all-to-all-done.2) | data formatting | bytes 12058624
  592.4 7.9 %copy.15 = bf16[1,512,5888]{2,1,0:T(8,128)(2,1)} copy(bf16[1,512,5888]{2,0,1:T(2,128)(2,1)} %bitcast.61) | data formatting | bytes 12058624
  (33 shorter events, 5.8 us)
Async XLA Ops:
  7.2 138.3 %all-to-all-start = ((bf16[16,32,5888]{2,1,0:T(8,128)(2,1)}), bf16[16,32,5888]{2,1,0:T(8,128)(2,1)}, u32[]{:S(2)}, u32[]{:S(2)}) async-start(bf16[16,32,5888]{2,1,0:T(8,128)(2,1)} %param.3), calls=%async_computation | async-start | bytes 12058624 | tf_op jit(solution)/shard_map/all_to_all | solution.py:15
  13.7 140.6 %all-gather.6.cloned.1.call-start = ((), (), s32[]{:S(2)}) async-start(), calls=%async_computation.7 | async-start | bytes 4521984 | tf_op jit(solution)/shard_map/all_gather | solution.py:23
  14.4 169.3 %all-reduce.3.cloned.1.call-start = ((), (), s32[]{:S(2)}) async-start(), calls=%async_computation.4 | async-start | bytes 524288 | tf_op jit(solution)/shard_map/psum | solution.py:26
  161.4 167.8 %reduce-scatter.2.cloned.1.call-start = ((), (), s32[]{:S(2)}) async-start(), calls=%async_computation.5 | async-start | bytes 9043968 | tf_op jit(solution)/shard_map/reduce_scatter | solution.py:33
  339.6 37.4 %copy-start = (bf16[1,2944,256]{2,1,0:T(8,128)(2,1)}, bf16[1,2944,256]{2,1,0:T(8,128)(2,1)S(1)}, u32[]{:S(2)}) copy-start(bf16[1,2944,256]{2,1,0:T(8,128)(2,1)S(1)} %get-tuple-element.21) | copy-start | bytes 4521988
  438.1 140.3 %all-to-all-start.2 = ((bf16[16,2,94208]{2,1,0:T(2,128)(2,1)}), bf16[16,2,94208]{2,1,0:T(2,128)(2,1)}, u32[]{:S(2)}, u32[]{:S(2)}) async-start(bf16[16,2,94208]{2,1,0:T(2,128)(2,1)} %reshape.63), calls=%async_computation.3 | async-start | bytes 12058624 | tf_op jit(solution)/shard_map/all_to_all | solution.py:63
  446.6 45.0 %all-gather.4.cloned.1.call-start = ((), (), s32[]{:S(2)}) async-start(), calls=%async_computation.6 | async-start | bytes 4521984 | tf_op jit(solution)/shard_map/all_gather | solution.py:43
Sparse Core Ops, SparseCore 0:
  16.0 43.8 all-gather.5
  161.5 22.1 all-reduce.2
  254.5 74.6 reduce-scatter.1
  448.6 42.9 all-gather.3
